TPU v7x, 512 devices: a whole 4x8x8 slice. The times are simulated.
512 devices in a mesh: sub: 16 (over z, core), blk: 32 (over x, y).
Axes of the slice: x: 4, y: 8, z: 8, core: 2. Of those that a mesh axis runs over, the one named last changes fastest.
Arguments:
- double_layer: bfloat16 [16, 2, 2048, 2048], P('sub', None, 'blk'), may hold values from -1 to 2
- single_layer: bfloat16 [16, 2, 2048, 2048], P('sub', None, 'blk'), may hold values from -1 to 2
- hypersingular: bfloat16 [16, 2, 2048, 2048], P('sub', None, 'blk'), may hold values from -1 to 2
- adjoint_double: bfloat16 [16, 2, 2048, 2048], P('sub', None, 'blk'), may hold values from -1 to 2
- matching: int32 [16, 1024], replicated, may hold values from 0 to 1023, each once within a row
- right_side: float32 [16, 2, 2, 2048, 64], P('sub', None, None, 'blk'), may hold values from -6 to 6
- start: float32 [16, 2, 2, 2048, 64], P('sub', None, None, 'blk'), may hold values from -4 to 4
Outputs:
- solution: float32 [16, 2, 2, 2048, 64], P('sub', None, None, 'blk')
Inputs may be any that keep to these rules, and one draw needn't show every extreme that they name: `matching`: each row is a permutation of 0 to 1023; row 0 pairs with no subdomain below and is not read.
All inputs are finite; a program needn't handle non-finite values.
Results may differ from a plain program's by a relative error of at most 0.015.
Values may be sent and summed in bfloat16 or wider, within the bound.
No kernel may reach another device: no remote copies, remote signals or barrier semaphores. Data moves between devices by JAX's collectives and lax.ppermute only.
A program may use at most 64 MiB of HBM per device.

v0:
```python
import jax
import jax.numpy as jnp
from jax import lax
from jax.sharding import Mesh
from jax.sharding import PartitionSpec as P

BASIS = 5
SUB = ("sub_0", "sub_1")
BLK = ("blk_0", "blk_1")
SUB_BLK = ("sub_0", "sub_1", "blk_0", "blk_1")
EPSILON = 1e-06


def passed_along(block, axis, distance):
    devices = range(lax.axis_size(axis))
    route = [(i - distance, i) for i in devices if i - distance in devices]
    return lax.ppermute(block, axis, route)


def copy_for_each(value, axis):
    peers = lax.axis_size(axis)
    return lax.all_to_all(
        jnp.broadcast_to(value[None], (peers, *value.shape)), axis, 0, 0, tiled=True
    )


def laid_out(blocks, dim):
    blocks = jnp.moveaxis(blocks, 0, dim)
    lengths = blocks.shape
    return blocks.reshape(*lengths[:dim], lengths[dim] * lengths[dim + 1], *lengths[dim + 2 :])


def gathered_copies(value, axis, dim):
    blocks = copy_for_each(value, axis)
    return laid_out(blocks, dim)


def over_axes(value, axes):
    for axis in axes:
        value = lax.psum(value, axis)
    return value


def complex_product(matrix, vector):
    width = vector.shape[-1] // 2
    count = matrix.shape[1]
    products = jnp.dot(
        matrix.reshape(2 * count, matrix.shape[2]), vector, preferred_element_type=jnp.float32
    )
    products = products.reshape(2, count, 2 * width)
    real_part = products[0, :, :width] - products[1, :, width:]
    imag_part = products[0, :, width:] + products[1, :, :width]
    return jnp.concatenate([real_part, imag_part], axis=-1)


def calderon(double_layer, single_layer, hypersingular, adjoint_double, vector):
    upper = complex_product(single_layer, vector[1]) - complex_product(double_layer, vector[0])
    lower = complex_product(hypersingular, vector[0]) + complex_product(adjoint_double, vector[1])
    return jnp.stack([upper, lower])


def inward(field):
    local_field = field[0]
    return jnp.concatenate([local_field[:, 0], local_field[:, 1]], axis=-1)


def outward(vector):
    width = vector.shape[-1] // 2
    return jnp.stack([vector[..., :width], vector[..., width:]], axis=1)[None]


def coupling_rows(gathered, matching, local_rows):
    subdomains = lax.axis_size(SUB)
    own_index = lax.axis_index(SUB)
    block_index = lax.axis_index(BLK)
    half_rows = local_rows // 2
    above_index = jnp.minimum(own_index + 1, subdomains - 1)
    perm_here = lax.dynamic_index_in_dim(matching, own_index, 0, keepdims=False)
    perm_above = lax.dynamic_index_in_dim(matching, above_index, 0, keepdims=False)
    window = block_index * half_rows
    odd_rows = gathered[:, 1::2]
    even_rows = gathered[:, 0::2]
    inverse_here = jnp.argsort(perm_here)
    send_upward = jnp.take(
        odd_rows, lax.dynamic_slice_in_dim(perm_above, window, half_rows), axis=1
    )
    send_downward = jnp.take(
        even_rows, lax.dynamic_slice_in_dim(inverse_here, window, half_rows), axis=1
    )
    lower_face = passed_along(send_upward, SUB, 1)
    upper_face = passed_along(send_downward, SUB, -1)
    joined = jnp.stack([lower_face, upper_face], axis=2)
    joined = joined.reshape(2, local_rows, gathered.shape[-1]).astype(jnp.float32)
    trace_signs = jnp.array([1.0, -1.0], jnp.float32).reshape(2, 1, 1)
    return joined * trace_signs


def preconditioned(operators, matching, vector):
    rounded = vector.astype(jnp.bfloat16)
    gathered = gathered_copies(rounded, BLK, 1)
    first_image = calderon(*operators, gathered)
    middle = first_image - 0.5 * coupling_rows(gathered, matching, vector.shape[1])
    middle_rounded = middle.astype(jnp.bfloat16)
    middle_full = gathered_copies(middle_rounded, BLK, 1)
    return calderon(*operators, middle_full)


def inner_local(first, second):
    totals = jnp.sum(first * second, axis=(0, 1))
    width = totals.shape[0] // 2
    return totals[:width] + totals[width:]


def spread(values):
    return jnp.concatenate([values, values])


def global_norm(vector):
    return jnp.sqrt(over_axes(inner_local(vector, vector), SUB_BLK) + EPSILON)


def body(double_layer, single_layer, hypersingular, adjoint_double, matching, right_side, start):
    operators = (double_layer[0], single_layer[0], hypersingular[0], adjoint_double[0])
    right_local = inward(right_side)
    start_local = inward(start)
    residual = right_local - preconditioned(operators, matching, start_local)
    beta = global_norm(residual)
    basis = [residual / spread(beta)]
    columns = []
    for column in range(BASIS):
        image = preconditioned(operators, matching, basis[column])
        local_dots = [inner_local(basis[earlier], image) for earlier in range(column + 1)]
        stacked_dots = jnp.stack(local_dots + [inner_local(image, image)])
        summed = over_axes(stacked_dots, SUB_BLK)
        coefficients = [summed[earlier] for earlier in range(column + 1)]
        for earlier in range(column + 1):
            image = image - spread(coefficients[earlier]) * basis[earlier]
        squares = summed[column + 1] - jnp.sum(summed[: column + 1] * summed[: column + 1], axis=0)
        height = jnp.sqrt(jnp.maximum(squares, 0.0) + EPSILON)
        if column + 1 < BASIS:
            basis.append(image / spread(height))
        filler = [jnp.zeros_like(height)] * (BASIS - 1 - column)
        columns.append(jnp.stack(coefficients + [height] + filler, axis=1))
    hessen = jnp.stack(columns, axis=2)
    gram = jnp.einsum("rij,rik->rjk", hessen, hessen, precision=lax.Precision.HIGHEST)
    target = beta[:, None] * hessen[:, 0, :]
    factor = jnp.linalg.cholesky(gram)
    weights = jax.scipy.linalg.cho_solve((factor, True), target[..., None])[..., 0]
    solution = start_local
    for column in range(BASIS):
        solution = solution + spread(weights[:, column]) * basis[column]
    return outward(solution)


def solution(mesh):
    torus = Mesh(mesh.devices.reshape(8, 2, 4, 8), ("sub_0", "sub_1", "blk_0", "blk_1"))
    placed = (
        P(SUB, None, BLK, None),
        P(SUB, None, BLK, None),
        P(SUB, None, BLK, None),
        P(SUB, None, BLK, None),
        P(),
        P(SUB, None, None, BLK, None),
        P(SUB, None, None, BLK, None),
    )
    return jax.shard_map(
        body, mesh=torus, in_specs=placed, out_specs=P(SUB, None, None, BLK, None), check_vma=False
    )
```

profile of v0, /device:TPU:2, one launch (start us, length us, event | category | flops | bytes accessed | tf_op | source)
XLA Modules:
  0.0 825.8 jit_solution(2891582693578804265)
XLA Ops:
  2.9 10.3 %all-to-all-start = ((bf16[32,2,64,128]{3,2,1,0:T(8,128)(2,1)}), bf16[32,2,64,128]{3,2,1,0:T(8,128)(2,1)S(1)}, u32[]{:S(2)}, u32[]{:S(2)}) async-start(bf16[32,2,64,128]{3,2,1,0:T(8,128)(2,1)} %broadcast_in_dim.37), calls=%async_computation | async-start | bytes 2097152 | tf_op jit(solution)/shard_map/all_to_all | solution.py:22
  13.9 4.4 sort.27
  19.2 20.1 %all-to-all-done = bf16[32,2,64,128]{3,2,1,0:T(8,128)(2,1)S(1)} async-done(((bf16[32,2,64,128]{3,2,1,0:T(8,128)(2,1)}), bf16[32,2,64,128]{3,2,1,0:T(8,128)(2,1)S(1)}, u32[]{:S(2)}, u32[]{:S(2)}) %all-to-all-start) | async-done | bytes 1048608 | tf_op jit(solution)/shard_map/all_to_all | solution.py:22
  39.3 1.6 slice.1012
  40.9 1.6 slice.1013
  46.3 1.3 collective-permute-start.1
  54.1 7.7 all-to-all-start.1
  61.9 24.3 %all-to-all-done.1 = bf16[32,2,64,128]{3,2,1,0:T(8,128)(2,1)S(1)} async-done(((bf16[32,2,64,128]{3,2,1,0:T(8,128)(2,1)}), bf16[32,2,64,128]{3,2,1,0:T(8,128)(2,1)S(1)}, u32[]{:S(2)}, u32[]{:S(2)}) %all-to-all-start.1) | async-done | bytes 1048608 | tf_op jit(solution)/shard_map/all_to_all | solution.py:22
  88.2 26.7 %psum.168 = f32[64]{0:T(128)S(1)} all-reduce(f32[64]{0:T(128)S(1)} %slice_add_fusion.48), channel_id=1, replica_groups=mesh['sub_0'=8,'sub_1'=2,'blk_0'=4,'blk_1'=8] {'sub_0'}, use_global_device_ids=true, to_apply=%region_2.4 | all-reduce | flops 64 | bytes 512 | tf_op jit(solution)/shard_map/psum | solution.py:40
  114.9 2.5 psum.169
  117.3 10.5 %psum.170 = f32[64]{0:T(128)S(1)} all-reduce(f32[64]{0:T(128)S(1)} %psum.169), channel_id=1, replica_groups=mesh['sub_0'=8,'sub_1'=2,'blk_0'=4,'blk_1'=8] {'blk_0'}, use_global_device_ids=true, to_apply=%region_4.6 | all-reduce | flops 64 | bytes 512 | tf_op jit(solution)/shard_map/psum | solution.py:40
  127.8 15.8 %psum.171 = f32[64]{0:T(128)S(1)} all-reduce(f32[64]{0:T(128)S(1)} %psum.170), channel_id=1, replica_groups=mesh['sub_0'=8,'sub_1'=2,'blk_0'=4,'blk_1'=8] {'blk_1'}, use_global_device_ids=true, to_apply=%region_5.7 | all-reduce | flops 64 | bytes 512 | tf_op jit(solution)/shard_map/psum | solution.py:40
  144.5 26.8 %all_to_all.60 = bf16[32,2,64,128]{3,2,1,0:T(8,128)(2,1)S(1)} all-to-all(bf16[32,2,64,128]{3,2,1,0:T(8,128)(2,1)S(1)} %broadcast_in_dim.39), channel_id=1, replica_groups=mesh['sub_0'=8,'sub_1'=2,'blk_0'=4,'blk_1'=8] {'blk_0','blk_1'}, dimensions={0} | all-to-all | bytes 2097152 | tf_op jit(solution)/shard_map/all_to_all | solution.py:22
  171.4 3.7 slice.1053
  175.0 3.6 slice.1052
  181.9 1.3 collective-permute-start.3
  184.5 3.0 collective-permute-start.2
  188.8 34.5 %all_to_all.61 = bf16[32,2,64,128]{3,2,1,0:T(8,128)(2,1)S(1)} all-to-all(bf16[32,2,64,128]{3,2,1,0:T(8,128)(2,1)S(1)} %broadcast_in_dim.40), channel_id=1, replica_groups=mesh['sub_0'=8,'sub_1'=2,'blk_0'=4,'blk_1'=8] {'blk_0','blk_1'}, dimensions={0} | all-to-all | bytes 2097152 | tf_op jit(solution)/shard_map/all_to_all | solution.py:22
  225.2 14.5 %psum.172 = f32[2,64]{1,0:T(2,128)S(1)} all-reduce(f32[2,64]{1,0:T(2,128)S(1)} %pad_maximum_fusion.8), channel_id=1, replica_groups=mesh['sub_0'=8,'sub_1'=2,'blk_0'=4,'blk_1'=8] {'sub_0'}, use_global_device_ids=true, to_apply=%region_8.10 | all-reduce | flops 128 | bytes 1024 | tf_op jit(solution)/shard_map/psum | solution.py:40
  239.8 2.5 psum.173
  242.2 10.4 %psum.174 = f32[2,64]{1,0:T(2,128)S(1)} all-reduce(f32[2,64]{1,0:T(2,128)S(1)} %psum.173), channel_id=1, replica_groups=mesh['sub_0'=8,'sub_1'=2,'blk_0'=4,'blk_1'=8] {'blk_0'}, use_global_device_ids=true, to_apply=%region_10.12 | all-reduce | flops 128 | bytes 1024 | tf_op jit(solution)/shard_map/psum | solution.py:40
  252.6 15.9 %psum.175 = f32[2,64]{1,0:T(2,128)S(1)} all-reduce(f32[2,64]{1,0:T(2,128)S(1)} %psum.174), channel_id=1, replica_groups=mesh['sub_0'=8,'sub_1'=2,'blk_0'=4,'blk_1'=8] {'blk_1'}, use_global_device_ids=true, to_apply=%region_11.13 | all-reduce | flops 128 | bytes 1024 | tf_op jit(solution)/shard_map/psum | solution.py:40
  270.0 26.8 %all_to_all.62 = bf16[32,2,64,128]{3,2,1,0:T(8,128)(2,1)S(1)} all-to-all(bf16[32,2,64,128]{3,2,1,0:T(8,128)(2,1)S(1)} %broadcast_in_dim.41), channel_id=1, replica_groups=mesh['sub_0'=8,'sub_1'=2,'blk_0'=4,'blk_1'=8] {'blk_0','blk_1'}, dimensions={0} | all-to-all | bytes 2097152 | tf_op jit(solution)/shard_map/all_to_all | solution.py:22
  296.9 3.7 slice.1097
  300.6 3.6 slice.1096
  307.5 1.4 fusion.18
  311.6 3.0 collective-permute-start.4
  316.5 34.5 %all_to_all.63 = bf16[32,2,64,128]{3,2,1,0:T(8,128)(2,1)S(1)} all-to-all(bf16[32,2,64,128]{3,2,1,0:T(8,128)(2,1)S(1)} %broadcast_in_dim.42), channel_id=1, replica_groups=mesh['sub_0'=8,'sub_1'=2,'blk_0'=4,'blk_1'=8] {'blk_0','blk_1'}, dimensions={0} | all-to-all | bytes 2097152 | tf_op jit(solution)/shard_map/all_to_all | solution.py:22
  353.1 15.5 %psum.176 = f32[3,64]{1,0:T(4,128)S(1)} all-reduce(f32[3,64]{1,0:T(4,128)S(1)} %pad_maximum_fusion.6), channel_id=1, replica_groups=mesh['sub_0'=8,'sub_1'=2,'blk_0'=4,'blk_1'=8] {'sub_0'}, use_global_device_ids=true, to_apply=%region_15.17 | all-reduce | flops 192 | bytes 1536 | tf_op jit(solution)/shard_map/psum | solution.py:40
  368.6 2.5 psum.177
  371.0 10.1 %psum.178 = f32[3,64]{1,0:T(4,128)S(1)} all-reduce(f32[3,64]{1,0:T(4,128)S(1)} %psum.177), channel_id=1, replica_groups=mesh['sub_0'=8,'sub_1'=2,'blk_0'=4,'blk_1'=8] {'blk_0'}, use_global_device_ids=true, to_apply=%region_17.19 | all-reduce | flops 192 | bytes 1536 | tf_op jit(solution)/shard_map/psum | solution.py:40
  381.1 16.3 %psum.179 = f32[3,64]{1,0:T(4,128)S(1)} all-reduce(f32[3,64]{1,0:T(4,128)S(1)} %psum.178), channel_id=1, replica_groups=mesh['sub_0'=8,'sub_1'=2,'blk_0'=4,'blk_1'=8] {'blk_1'}, use_global_device_ids=true, to_apply=%region_18.20 | all-reduce | flops 192 | bytes 1536 | tf_op jit(solution)/shard_map/psum | solution.py:40
  399.0 27.0 %all_to_all.64 = bf16[32,2,64,128]{3,2,1,0:T(8,128)(2,1)S(1)} all-to-all(bf16[32,2,64,128]{3,2,1,0:T(8,128)(2,1)S(1)} %broadcast_in_dim.43), channel_id=1, replica_groups=mesh['sub_0'=8,'sub_1'=2,'blk_0'=4,'blk_1'=8] {'blk_0','blk_1'}, dimensions={0} | all-to-all | bytes 2097152 | tf_op jit(solution)/shard_map/all_to_all | solution.py:22
  426.0 3.7 slice.1145
  429.7 3.6 slice.1144
  437.2 1.4 fusion.19
  441.4 3.0 collective-permute-start.6
  446.8 33.8 %all_to_all.65 = bf16[32,2,64,128]{3,2,1,0:T(8,128)(2,1)S(1)} all-to-all(bf16[32,2,64,128]{3,2,1,0:T(8,128)(2,1)S(1)} %broadcast_in_dim.44), channel_id=1, replica_groups=mesh['sub_0'=8,'sub_1'=2,'blk_0'=4,'blk_1'=8] {'blk_0','blk_1'}, dimensions={0} | all-to-all | bytes 2097152 | tf_op jit(solution)/shard_map/all_to_all | solution.py:22
  482.7 15.8 %psum.180 = f32[4,64]{1,0:T(4,128)S(1)} all-reduce(f32[4,64]{1,0:T(4,128)S(1)} %pad_maximum_fusion.7), channel_id=1, replica_groups=mesh['sub_0'=8,'sub_1'=2,'blk_0'=4,'blk_1'=8] {'sub_0'}, use_global_device_ids=true, to_apply=%region_24.26 | all-reduce | flops 256 | bytes 2048 | tf_op jit(solution)/shard_map/psum | solution.py:40
  498.6 2.5 psum.181
  501.0 10.5 %psum.182 = f32[4,64]{1,0:T(4,128)S(1)} all-reduce(f32[4,64]{1,0:T(4,128)S(1)} %psum.181), channel_id=1, replica_groups=mesh['sub_0'=8,'sub_1'=2,'blk_0'=4,'blk_1'=8] {'blk_0'}, use_global_device_ids=true, to_apply=%region_26.28 | all-reduce | flops 256 | bytes 2048 | tf_op jit(solution)/shard_map/psum | solution.py:40
  511.5 15.8 %psum.183 = f32[4,64]{1,0:T(4,128)S(1)} all-reduce(f32[4,64]{1,0:T(4,128)S(1)} %psum.182), channel_id=1, replica_groups=mesh['sub_0'=8,'sub_1'=2,'blk_0'=4,'blk_1'=8] {'blk_1'}, use_global_device_ids=true, to_apply=%region_27.29 | all-reduce | flops 256 | bytes 2048 | tf_op jit(solution)/shard_map/psum | solution.py:40
  528.8 26.8 %all_to_all.66 = bf16[32,2,64,128]{3,2,1,0:T(8,128)(2,1)S(1)} all-to-all(bf16[32,2,64,128]{3,2,1,0:T(8,128)(2,1)S(1)} %broadcast_in_dim.45), channel_id=1, replica_groups=mesh['sub_0'=8,'sub_1'=2,'blk_0'=4,'blk_1'=8] {'blk_0','blk_1'}, dimensions={0} | all-to-all | bytes 2097152 | tf_op jit(solution)/shard_map/all_to_all | solution.py:22
  555.7 3.7 slice.1196
  559.3 3.6 slice.1195
  567.5 1.4 fusion.20
  571.7 3.0 collective-permute-start.8
  577.8 33.7 %all_to_all.67 = bf16[32,2,64,128]{3,2,1,0:T(8,128)(2,1)S(1)} all-to-all(bf16[32,2,64,128]{3,2,1,0:T(8,128)(2,1)S(1)} %broadcast_in_dim.46), channel_id=1, replica_groups=mesh['sub_0'=8,'sub_1'=2,'blk_0'=4,'blk_1'=8] {'blk_0','blk_1'}, dimensions={0} | all-to-all | bytes 2097152 | tf_op jit(solution)/shard_map/all_to_all | solution.py:22
  613.8 15.9 %psum.184 = f32[5,64]{1,0:T(8,128)S(1)} all-reduce(f32[5,64]{1,0:T(8,128)S(1)} %stack.288), channel_id=1, replica_groups=mesh['sub_0'=8,'sub_1'=2,'blk_0'=4,'blk_1'=8] {'sub_0'}, use_global_device_ids=true, to_apply=%region_34.36 | all-reduce | flops 320 | bytes 2560 | tf_op jit(solution)/shard_map/psum | solution.py:40
  629.7 2.5 psum.185
  632.1 10.4 %psum.186 = f32[5,64]{1,0:T(8,128)S(1)} all-reduce(f32[5,64]{1,0:T(8,128)S(1)} %psum.185), channel_id=1, replica_groups=mesh['sub_0'=8,'sub_1'=2,'blk_0'=4,'blk_1'=8] {'blk_0'}, use_global_device_ids=true, to_apply=%region_36.38 | all-reduce | flops 320 | bytes 2560 | tf_op jit(solution)/shard_map/psum | solution.py:40
  642.6 15.7 %psum.187 = f32[5,64]{1,0:T(8,128)S(1)} all-reduce(f32[5,64]{1,0:T(8,128)S(1)} %psum.186), channel_id=1, replica_groups=mesh['sub_0'=8,'sub_1'=2,'blk_0'=4,'blk_1'=8] {'blk_1'}, use_global_device_ids=true, to_apply=%region_37.39 | all-reduce | flops 320 | bytes 2560 | tf_op jit(solution)/shard_map/psum | solution.py:40
  660.4 27.0 %all_to_all.68 = bf16[32,2,64,128]{3,2,1,0:T(8,128)(2,1)S(1)} all-to-all(bf16[32,2,64,128]{3,2,1,0:T(8,128)(2,1)S(1)} %broadcast_in_dim.47), channel_id=1, replica_groups=mesh['sub_0'=8,'sub_1'=2,'blk_0'=4,'blk_1'=8] {'blk_0','blk_1'}, dimensions={0} | all-to-all | bytes 2097152 | tf_op jit(solution)/shard_map/all_to_all | solution.py:22
  687.5 3.7 slice.1250
  691.2 3.6 slice.1249
  699.3 1.4 fusion.21
  703.5 3.2 collective-permute-start.10
  710.9 7.7 all-to-all-start.11
  725.5 19.4 %all-to-all-done.11 = bf16[32,2,64,128]{3,2,1,0:T(8,128)(2,1)S(1)} async-done(((bf16[32,2,64,128]{3,2,1,0:T(8,128)(2,1)}), bf16[32,2,64,128]{3,2,1,0:T(8,128)(2,1)S(1)}, u32[]{:S(2)}, u32[]{:S(2)}) %all-to-all-start.11) | async-done | bytes 1048608 | tf_op jit(solution)/shard_map/all_to_all | solution.py:22
  747.9 15.7 %psum.188 = f32[6,64]{1,0:T(8,128)S(1)} all-reduce(f32[6,64]{1,0:T(8,128)S(1)} %stack.302), channel_id=1, replica_groups=mesh['sub_0'=8,'sub_1'=2,'blk_0'=4,'blk_1'=8] {'sub_0'}, use_global_device_ids=true, to_apply=%region_45.47 | all-reduce | flops 384 | bytes 3072 | tf_op jit(solution)/shard_map/psum | solution.py:40
  763.6 2.5 psum.189
  766.1 10.4 %psum.190 = f32[6,64]{1,0:T(8,128)S(1)} all-reduce(f32[6,64]{1,0:T(8,128)S(1)} %psum.189), channel_id=1, replica_groups=mesh['sub_0'=8,'sub_1'=2,'blk_0'=4,'blk_1'=8] {'blk_0'}, use_global_device_ids=true, to_apply=%region_47.49 | all-reduce | flops 384 | bytes 3072 | tf_op jit(solution)/shard_map/psum | solution.py:40
  776.5 15.7 %psum.191 = f32[6,64]{1,0:T(8,128)S(1)} all-reduce(f32[6,64]{1,0:T(8,128)S(1)} %psum.190), channel_id=1, replica_groups=mesh['sub_0'=8,'sub_1'=2,'blk_0'=4,'blk_1'=8] {'blk_1'}, use_global_device_ids=true, to_apply=%region_48.50 | all-reduce | flops 384 | bytes 3072 | tf_op jit(solution)/shard_map/psum | solution.py:40
  794.2 29.4 %custom-call.11 = f32[64,5,5]{2,1,0:T(8,128)S(1)} custom-call(f32[64,5,5]{2,1,0:T(8,128)S(1)} %fusion), custom_call_target="Cholesky" | custom-call | tf_op jit(solution)/shard_map/jit(cholesky)/cholesky | solution.py:147
  (465 shorter events, 89.9 us)
Async XLA Ops:
  0.0 50.0 %copy-start = (bf16[1,2,64,2048]{3,2,1,0:T(8,128)(2,1)S(1)}, bf16[1,2,64,2048]{3,2,1,0:T(8,128)(2,1)}, u32[]{:S(2)}) copy-start(bf16[1,2,64,2048]{3,2,1,0:T(8,128)(2,1)} %param.16) | copy-start | bytes 1572868
  1.0 0.6 copy-start.21
  2.9 36.4 %all-to-all-start = ((bf16[32,2,64,128]{3,2,1,0:T(8,128)(2,1)}), bf16[32,2,64,128]{3,2,1,0:T(8,128)(2,1)S(1)}, u32[]{:S(2)}, u32[]{:S(2)}) async-start(bf16[32,2,64,128]{3,2,1,0:T(8,128)(2,1)} %broadcast_in_dim.37), calls=%async_computation | async-start | bytes 2097152 | tf_op jit(solution)/shard_map/all_to_all | solution.py:22
  18.4 163.4 %copy-start.30 = (pred[32]{0:T(512)(128)(4,1)}, pred[32]{0:T(512)(128)(4,1)S(1)}, u32[]{:S(2)}) copy-start(pred[32]{0:T(512)(128)(4,1)S(1)} %get-tuple-element.40) | copy-start | bytes 100
  19.2 165.2 %copy-start.25 = (pred[32]{0:T(512)(128)(4,1)}, pred[32]{0:T(512)(128)(4,1)S(1)}, u32[]{:S(2)}) copy-start(pred[32]{0:T(512)(128)(4,1)S(1)} %get-tuple-element.38) | copy-start | bytes 100
  19.2 162.0 %copy-start.39 = (s32[1024]{0:T(1024)}, s32[1024]{0:T(1024)S(1)}, u32[]{:S(2)}) copy-start(s32[1024]{0:T(1024)S(1)} %get-tuple-element.215) | copy-start | bytes 12292
  19.2 164.6 %copy-start.38 = (s32[1024]{0:T(1024)}, s32[1024]{0:T(1024)S(1)}, u32[]{:S(2)}) copy-start(s32[1024]{0:T(1024)S(1)} %get-tuple-element.216) | copy-start | bytes 12292
  43.7 8.0 collective-permute-start
  46.3 5.7 collective-permute-start.1
  47.6 1.0 copy-start.2
  48.6 1.0 copy-start.3
  50.0 1.0 copy-start.1
  52.1 0.7 copy-start.31
  54.0 7.8 copy-start.24
  54.1 32.1 %all-to-all-start.1 = ((bf16[32,2,64,128]{3,2,1,0:T(8,128)(2,1)}), bf16[32,2,64,128]{3,2,1,0:T(8,128)(2,1)S(1)}, u32[]{:S(2)}, u32[]{:S(2)}) async-start(bf16[32,2,64,128]{3,2,1,0:T(8,128)(2,1)} %broadcast_in_dim.38), calls=%async_computation.1 | async-start | bytes 2097152 | tf_op jit(solution)/shard_map/all_to_all | solution.py:22
  179.6 1.0 copy-start.9
  180.7 2.6 copy-start.5
  181.9 6.2 collective-permute-start.3
  184.5 3.9 collective-permute-start.2
  305.2 1.0 copy-start.10
  306.2 3.9 copy-start.6
  308.9 6.3 collective-permute-start.5
  310.7 0.7 copy-start.26
  311.6 3.9 collective-permute-start.4
  315.5 0.7 copy-start.32
  397.4 0.8 copy-start.40
  434.9 1.0 copy-start.11
  435.9 3.9 copy-start.7
  438.6 6.4 collective-permute-start.7
  439.9 1.4 copy-start.27
  440.4 4.0 copy-start.17
  441.4 4.3 collective-permute-start.6
  445.8 0.7 copy-start.33
  527.3 0.8 copy-start.37
  565.2 1.0 copy-start.12
  566.2 3.9 copy-start.8
  568.8 7.2 collective-permute-start.9
  570.1 1.4 copy-start.28
  570.7 4.0 copy-start.18
  571.7 5.1 collective-permute-start.8
  574.7 0.8 copy-start.15
  576.9 0.7 copy-start.34
  658.2 0.9 copy-start.36
  697.0 1.0 copy-start.13
  698.1 3.9 copy-start.4
  700.7 7.4 collective-permute-start.11
  702.0 1.4 copy-start.29
  702.5 4.2 copy-start.16
  703.5 5.3 collective-permute-start.10
  706.8 0.8 copy-start.14
  708.9 0.7 copy-start.35
  710.9 34.0 %all-to-all-start.11 = ((bf16[32,2,64,128]{3,2,1,0:T(8,128)(2,1)}), bf16[32,2,64,128]{3,2,1,0:T(8,128)(2,1)S(1)}, u32[]{:S(2)}, u32[]{:S(2)}) async-start(bf16[32,2,64,128]{3,2,1,0:T(8,128)(2,1)} %broadcast_in_dim.48), calls=%async_computation.11 | async-start | bytes 2097152 | tf_op jit(solution)/shard_map/all_to_all | solution.py:22
  718.7 0.7 copy-start.52
  719.4 0.7 copy-start.60
  719.4 5.4 copy-start.47
  720.7 0.7 copy-start.49
  723.4 0.7 copy-start.58
  724.8 0.7 copy-start.44
  724.8 0.7 copy-start.45
  724.8 0.7 copy-start.46
  746.6 0.8 copy-start.23
  792.3 0.7 copy-start.54
  823.8 0.9 copy-start.22
  823.8 0.9 copy-start.20
  (12 other events, 7.3 us)
where the time goes:
time: 836 us; the launch traced here: 826 us
  blocking collectives  547 us (65%)
  local copies, waits for them, and re-layouts  88.4 us (11%)
  waiting for transfers between devices  64.6 us (8%)
  other arithmetic  55.6 us (7%)
  starting transfers between devices  50.1 us (6%)
  matrix products  17.5 us (2%)
    psum x24, blocking collectives, over_axes(): value = lax.psum(value, axis)  276 us
    all_to_all x9, blocking collectives, copy_for_each(): lax.all_to_all(jnp.broadcast_to(value[None], (peers, *value.shape)), axis...  271 us
    all_to_all x3, waiting for transfers between devices, copy_for_each(): lax.all_to_all(jnp.broadcast_to(value[None], (peers, *value.shape)), axis...  63.8 us
    another operation x4, other arithmetic, body(): factor = jnp.linalg.cholesky(gram)  29.5 us
    unnamed x139, local copies, waits for them, and re-layouts  26.8 us
    all_to_all x3, starting transfers between devices, copy_for_each(): lax.all_to_all(jnp.broadcast_to(value[None], (peers, *value.shape)), axis...  25.7 us
    ppermute x12, starting transfers between devices, passed_along(): return lax.ppermute(block, axis, route)  24.4 us
    slice x6, local copies, waits for them, and re-layouts, coupling_rows(): even_rows = gathered[:, 0::2]  19.9 us
  transfers between devices with their start and end apart: 15, of which 6 were waited for; matrix products, arithmetic and copies ran while one was open for 3% of the time, Pallas kernels for 0%

commit v1 on v0

--- a/solution.py
+++ b/solution.py
@@ -37,7 +37,8 @@
 
 def over_axes(value, axes):
     for axis in axes:
-        value = lax.psum(value, axis)
+        pieces = lax.all_gather(value, axis, axis=0, tiled=False)
+        value = pieces.sum(axis=0)
     return value
 
 

time: 836 us -> 894 us (1.069)
  the two profiles are of different devices: /device:TPU:2 before, /device:TPU:8 now
where the time goes in v1:
time: 894 us; the launch traced here: 883 us
  blocking collectives  599 us (67%)
  local copies, waits for them, and re-layouts  94.7 us (11%)
  waiting for transfers between devices  64.4 us (7%)
  other arithmetic  56.1 us (6%)
  starting transfers between devices  45.7 us (5%)
  matrix products  17.5 us (2%)
    all_to_all x9, blocking collectives, copy_for_each(): lax.all_to_all(jnp.broadcast_to(value[None], (peers, *value.shape)), axis...  276 us
    all_gather x20, blocking collectives, over_axes(): pieces = lax.all_gather(value, axis, axis=0, tiled=False)  272 us
    all_to_all x3, waiting for transfers between devices, copy_for_each(): lax.all_to_all(jnp.broadcast_to(value[None], (peers, *value.shape)), axis...  63.6 us
    unnamed x4, blocking collectives  51.8 us
    unnamed x150, local copies, waits for them, and re-layouts  32.7 us
    another operation x4, other arithmetic, body(): factor = jnp.linalg.cholesky(gram)  29.5 us
    ppermute x12, starting transfers between devices, passed_along(): return lax.ppermute(block, axis, route)  24.5 us
    all_to_all x3, starting transfers between devices, copy_for_each(): lax.all_to_all(jnp.broadcast_to(value[None], (peers, *value.shape)), axis...  21.2 us
  transfers between devices with their start and end apart: 15, of which 6 were waited for; matrix products, arithmetic and copies ran while one was open for 3% of the time, Pallas kernels for 0%

profile of v1, /device:TPU:8, one launch (start us, length us, event | category | flops | bytes accessed | tf_op | source)
XLA Modules:
  0.0 882.8 jit_solution(3531138959713462353)
XLA Ops:
  2.9 10.2 %all-to-all-start = ((bf16[32,2,64,128]{3,2,1,0:T(8,128)(2,1)}), bf16[32,2,64,128]{3,2,1,0:T(8,128)(2,1)S(1)}, u32[]{:S(2)}, u32[]{:S(2)}) async-start(bf16[32,2,64,128]{3,2,1,0:T(8,128)(2,1)} %broadcast_in_dim.37), calls=%async_computation | async-start | bytes 2097152 | tf_op jit(solution)/shard_map/all_to_all | solution.py:22
  13.9 4.4 sort.27
  19.1 22.5 %all-to-all-done = bf16[32,2,64,128]{3,2,1,0:T(8,128)(2,1)S(1)} async-done(((bf16[32,2,64,128]{3,2,1,0:T(8,128)(2,1)}), bf16[32,2,64,128]{3,2,1,0:T(8,128)(2,1)S(1)}, u32[]{:S(2)}, u32[]{:S(2)}) %all-to-all-start) | async-done | bytes 1048608 | tf_op jit(solution)/shard_map/all_to_all | solution.py:22
  41.7 1.6 slice.1012
  43.2 1.6 slice.1013
  56.4 5.3 all-to-all-start.1
  63.0 1.3 dynamic-slice.2
  69.5 19.3 %all-to-all-done.1 = bf16[32,2,64,128]{3,2,1,0:T(8,128)(2,1)S(1)} async-done(((bf16[32,2,64,128]{3,2,1,0:T(8,128)(2,1)}), bf16[32,2,64,128]{3,2,1,0:T(8,128)(2,1)S(1)}, u32[]{:S(2)}, u32[]{:S(2)}) %all-to-all-start.1) | async-done | bytes 1048608 | tf_op jit(solution)/shard_map/all_to_all | solution.py:22
  90.9 26.4 %all-reduce = f32[512]{0:T(512)S(1)} all-reduce(f32[512]{0:T(512)S(1)} %add_dynamic-update-slice_fusion), channel_id=2, replica_groups=mesh['sub_0'=8,'sub_1'=2,'blk_0'=4,'blk_1'=8] {'sub_0'}, use_global_device_ids=true, to_apply=%add | all-reduce | flops 512 | bytes 4096
  117.6 2.4 all-reduce.1
  120.4 8.9 %all-reduce.2 = f32[256]{0:T(256)S(1)} all-reduce(f32[256]{0:T(256)S(1)} %dynamic-update-slice.5), channel_id=4, replica_groups=mesh['sub_0'=8,'sub_1'=2,'blk_0'=4,'blk_1'=8] {'blk_0'}, use_global_device_ids=true, to_apply=%add.2 | all-reduce | flops 256 | bytes 2048
  129.6 14.1 %all-reduce.3 = f32[512]{0:T(512)S(1)} all-reduce(f32[512]{0:T(512)S(1)} %dynamic-update-slice.6), channel_id=5, replica_groups=mesh['sub_0'=8,'sub_1'=2,'blk_0'=4,'blk_1'=8] {'blk_1'}, use_global_device_ids=true, to_apply=%add.3 | all-reduce | flops 512 | bytes 4096
  144.8 30.0 %all_to_all.60 = bf16[32,2,64,128]{3,2,1,0:T(8,128)(2,1)S(1)} all-to-all(bf16[32,2,64,128]{3,2,1,0:T(8,128)(2,1)S(1)} %broadcast_in_dim.39), channel_id=1, replica_groups=mesh['sub_0'=8,'sub_1'=2,'blk_0'=4,'blk_1'=8] {'blk_0','blk_1'}, dimensions={0} | all-to-all | bytes 2097152 | tf_op jit(solution)/shard_map/all_to_all | solution.py:22
  174.9 3.7 slice.1053
  178.6 3.6 slice.1052
  188.1 3.0 collective-permute-start.2
  192.3 33.6 %all_to_all.65 = bf16[32,2,64,128]{3,2,1,0:T(8,128)(2,1)S(1)} all-to-all(bf16[32,2,64,128]{3,2,1,0:T(8,128)(2,1)S(1)} %broadcast_in_dim.40), channel_id=1, replica_groups=mesh['sub_0'=8,'sub_1'=2,'blk_0'=4,'blk_1'=8] {'blk_0','blk_1'}, dimensions={0} | all-to-all | bytes 2097152 | tf_op jit(solution)/shard_map/all_to_all | solution.py:22
  227.9 14.2 %all-gather.24 = f32[8,2,64]{2,1,0:T(2,128)S(1)} all-gather(f32[1,2,64]{2,1,0:T(2,128)S(1)} %maximum_bitcast_fusion.4), channel_id=6, replica_groups=mesh['sub_0'=8,'sub_1'=2,'blk_0'=4,'blk_1'=8] {'sub_0'}, dimensions={0}, use_global_device_ids=true | all-gather | bytes 4608 | tf_op jit(solution)/shard_map/all_gather | solution.py:40
  242.1 1.8 all-gather.25
  244.0 8.2 all-gather.26
  252.1 13.1 %all-gather.27 = f32[8,2,64]{2,1,0:T(2,128)S(1)} all-gather(f32[1,2,64]{2,1,0:T(2,128)S(1)} %bitcast.827), channel_id=9, replica_groups=mesh['sub_0'=8,'sub_1'=2,'blk_0'=4,'blk_1'=8] {'blk_1'}, dimensions={0}, use_global_device_ids=true | all-gather | bytes 4608 | tf_op jit(solution)/shard_map/all_gather | solution.py:40
  266.7 30.3 %all_to_all.61 = bf16[32,2,64,128]{3,2,1,0:T(8,128)(2,1)S(1)} all-to-all(bf16[32,2,64,128]{3,2,1,0:T(8,128)(2,1)S(1)} %broadcast_in_dim.41), channel_id=1, replica_groups=mesh['sub_0'=8,'sub_1'=2,'blk_0'=4,'blk_1'=8] {'blk_0','blk_1'}, dimensions={0} | all-to-all | bytes 2097152 | tf_op jit(solution)/shard_map/all_to_all | solution.py:22
  297.1 3.7 slice.1097
  300.7 3.6 slice.1096
  307.6 1.4 fusion.18
  311.7 3.0 collective-permute-start.4
  316.6 34.7 %all_to_all.66 = bf16[32,2,64,128]{3,2,1,0:T(8,128)(2,1)S(1)} all-to-all(bf16[32,2,64,128]{3,2,1,0:T(8,128)(2,1)S(1)} %broadcast_in_dim.42), channel_id=1, replica_groups=mesh['sub_0'=8,'sub_1'=2,'blk_0'=4,'blk_1'=8] {'blk_0','blk_1'}, dimensions={0} | all-to-all | bytes 2097152 | tf_op jit(solution)/shard_map/all_to_all | solution.py:22
  353.4 22.4 %all-gather.28 = f32[8,3,64]{2,1,0:T(4,128)S(1)} all-gather(f32[1,3,64]{2,1,0:T(4,128)S(1)} %maximum_bitcast_fusion.2), channel_id=10, replica_groups=mesh['sub_0'=8,'sub_1'=2,'blk_0'=4,'blk_1'=8] {'sub_0'}, dimensions={0}, use_global_device_ids=true | all-gather | bytes 6912 | tf_op jit(solution)/shard_map/all_gather | solution.py:40
  375.8 1.8 all-gather.29
  377.6 10.4 %all-gather.30 = f32[4,3,64]{2,1,0:T(4,128)S(1)} all-gather(f32[1,3,64]{2,1,0:T(4,128)S(1)} %bitcast.821), channel_id=12, replica_groups=mesh['sub_0'=8,'sub_1'=2,'blk_0'=4,'blk_1'=8] {'blk_0'}, dimensions={0}, use_global_device_ids=true | all-gather | bytes 3840 | tf_op jit(solution)/shard_map/all_gather | solution.py:40
  388.1 21.0 %all-gather.31 = f32[8,3,64]{2,1,0:T(4,128)S(1)} all-gather(f32[1,3,64]{2,1,0:T(4,128)S(1)} %bitcast.823), channel_id=13, replica_groups=mesh['sub_0'=8,'sub_1'=2,'blk_0'=4,'blk_1'=8] {'blk_1'}, dimensions={0}, use_global_device_ids=true | all-gather | bytes 6912 | tf_op jit(solution)/shard_map/all_gather | solution.py:40
  410.7 26.7 %all_to_all.62 = bf16[32,2,64,128]{3,2,1,0:T(8,128)(2,1)S(1)} all-to-all(bf16[32,2,64,128]{3,2,1,0:T(8,128)(2,1)S(1)} %broadcast_in_dim.43), channel_id=1, replica_groups=mesh['sub_0'=8,'sub_1'=2,'blk_0'=4,'blk_1'=8] {'blk_0','blk_1'}, dimensions={0} | all-to-all | bytes 2097152 | tf_op jit(solution)/shard_map/all_to_all | solution.py:22
  437.4 3.7 slice.1145
  441.1 3.6 slice.1144
  448.6 1.4 fusion.19
  452.8 3.2 collective-permute-start.6
  458.4 33.9 %all_to_all.67 = bf16[32,2,64,128]{3,2,1,0:T(8,128)(2,1)S(1)} all-to-all(bf16[32,2,64,128]{3,2,1,0:T(8,128)(2,1)S(1)} %broadcast_in_dim.44), channel_id=1, replica_groups=mesh['sub_0'=8,'sub_1'=2,'blk_0'=4,'blk_1'=8] {'blk_0','blk_1'}, dimensions={0} | all-to-all | bytes 2097152 | tf_op jit(solution)/shard_map/all_to_all | solution.py:22
  494.5 21.3 %all-gather.32 = f32[8,4,64]{2,1,0:T(4,128)S(1)} all-gather(f32[1,4,64]{2,1,0:T(4,128)S(1)} %maximum_bitcast_fusion.3), channel_id=14, replica_groups=mesh['sub_0'=8,'sub_1'=2,'blk_0'=4,'blk_1'=8] {'sub_0'}, dimensions={0}, use_global_device_ids=true | all-gather | bytes 9216 | tf_op jit(solution)/shard_map/all_gather | solution.py:40
  515.9 1.8 all-gather.33
  517.7 10.4 %all-gather.34 = f32[4,4,64]{2,1,0:T(4,128)S(1)} all-gather(f32[1,4,64]{2,1,0:T(4,128)S(1)} %bitcast.822), channel_id=16, replica_groups=mesh['sub_0'=8,'sub_1'=2,'blk_0'=4,'blk_1'=8] {'blk_0'}, dimensions={0}, use_global_device_ids=true | all-gather | bytes 5120 | tf_op jit(solution)/shard_map/all_gather | solution.py:40
  528.2 21.0 %all-gather.35 = f32[8,4,64]{2,1,0:T(4,128)S(1)} all-gather(f32[1,4,64]{2,1,0:T(4,128)S(1)} %bitcast.824), channel_id=17, replica_groups=mesh['sub_0'=8,'sub_1'=2,'blk_0'=4,'blk_1'=8] {'blk_1'}, dimensions={0}, use_global_device_ids=true | all-gather | bytes 9216 | tf_op jit(solution)/shard_map/all_gather | solution.py:40
  550.7 26.8 %all_to_all.63 = bf16[32,2,64,128]{3,2,1,0:T(8,128)(2,1)S(1)} all-to-all(bf16[32,2,64,128]{3,2,1,0:T(8,128)(2,1)S(1)} %broadcast_in_dim.45), channel_id=1, replica_groups=mesh['sub_0'=8,'sub_1'=2,'blk_0'=4,'blk_1'=8] {'blk_0','blk_1'}, dimensions={0} | all-to-all | bytes 2097152 | tf_op jit(solution)/shard_map/all_to_all | solution.py:22
  577.6 3.7 slice.1196
  581.2 3.6 slice.1195
  589.4 1.4 fusion.20
  593.6 3.0 collective-permute-start.8
  599.7 34.7 %all_to_all.68 = bf16[32,2,64,128]{3,2,1,0:T(8,128)(2,1)S(1)} all-to-all(bf16[32,2,64,128]{3,2,1,0:T(8,128)(2,1)S(1)} %broadcast_in_dim.46), channel_id=1, replica_groups=mesh['sub_0'=8,'sub_1'=2,'blk_0'=4,'blk_1'=8] {'blk_0','blk_1'}, dimensions={0} | all-to-all | bytes 2097152 | tf_op jit(solution)/shard_map/all_to_all | solution.py:22
  636.7 24.7 %all-gather.36 = f32[8,5,64]{2,1,0:T(8,128)S(1)} all-gather(f32[1,5,64]{2,1,0:T(8,128)S(1)} %bitcast.815), channel_id=18, replica_groups=mesh['sub_0'=8,'sub_1'=2,'blk_0'=4,'blk_1'=8] {'sub_0'}, dimensions={0}, use_global_device_ids=true | all-gather | bytes 11520 | tf_op jit(solution)/shard_map/all_gather | solution.py:40
  661.4 1.8 all-gather.37
  663.2 12.0 %all-gather.38 = f32[4,5,64]{2,1,0:T(8,128)S(1)} all-gather(f32[1,5,64]{2,1,0:T(8,128)S(1)} %bitcast.811), channel_id=20, replica_groups=mesh['sub_0'=8,'sub_1'=2,'blk_0'=4,'blk_1'=8] {'blk_0'}, dimensions={0}, use_global_device_ids=true | all-gather | bytes 6400 | tf_op jit(solution)/shard_map/all_gather | solution.py:40
  675.2 23.5 %all-gather.39 = f32[8,5,64]{2,1,0:T(8,128)S(1)} all-gather(f32[1,5,64]{2,1,0:T(8,128)S(1)} %bitcast.817), channel_id=21, replica_groups=mesh['sub_0'=8,'sub_1'=2,'blk_0'=4,'blk_1'=8] {'blk_1'}, dimensions={0}, use_global_device_ids=true | all-gather | bytes 11520 | tf_op jit(solution)/shard_map/all_gather | solution.py:40
  700.9 25.4 %all_to_all.64 = bf16[32,2,64,128]{3,2,1,0:T(8,128)(2,1)S(1)} all-to-all(bf16[32,2,64,128]{3,2,1,0:T(8,128)(2,1)S(1)} %broadcast_in_dim.47), channel_id=1, replica_groups=mesh['sub_0'=8,'sub_1'=2,'blk_0'=4,'blk_1'=8] {'blk_0','blk_1'}, dimensions={0} | all-to-all | bytes 2097152 | tf_op jit(solution)/shard_map/all_to_all | solution.py:22
  726.4 3.7 slice.1250
  730.1 3.6 slice.1249
  738.2 1.4 fusion.21
  739.5 1.5 collective-permute-start.11
  742.6 3.0 collective-permute-start.10
  749.7 5.7 all-to-all-start.11
  762.3 21.8 %all-to-all-done.11 = bf16[32,2,64,128]{3,2,1,0:T(8,128)(2,1)S(1)} async-done(((bf16[32,2,64,128]{3,2,1,0:T(8,128)(2,1)}), bf16[32,2,64,128]{3,2,1,0:T(8,128)(2,1)S(1)}, u32[]{:S(2)}, u32[]{:S(2)}) %all-to-all-start.11) | async-done | bytes 1048608 | tf_op jit(solution)/shard_map/all_to_all | solution.py:22
  787.2 24.7 %all-gather.40 = f32[8,6,64]{2,1,0:T(8,128)S(1)} all-gather(f32[1,6,64]{2,1,0:T(8,128)S(1)} %bitcast.814), channel_id=22, replica_groups=mesh['sub_0'=8,'sub_1'=2,'blk_0'=4,'blk_1'=8] {'sub_0'}, dimensions={0}, use_global_device_ids=true | all-gather | bytes 13824 | tf_op jit(solution)/shard_map/all_gather | solution.py:40
  811.9 1.8 all-gather.41
  813.7 12.0 %all-gather.42 = f32[4,6,64]{2,1,0:T(8,128)S(1)} all-gather(f32[1,6,64]{2,1,0:T(8,128)S(1)} %bitcast.813), channel_id=24, replica_groups=mesh['sub_0'=8,'sub_1'=2,'blk_0'=4,'blk_1'=8] {'blk_0'}, dimensions={0}, use_global_device_ids=true | all-gather | bytes 7680 | tf_op jit(solution)/shard_map/all_gather | solution.py:40
  825.7 23.5 %all-gather.43 = f32[8,6,64]{2,1,0:T(8,128)S(1)} all-gather(f32[1,6,64]{2,1,0:T(8,128)S(1)} %bitcast.818), channel_id=25, replica_groups=mesh['sub_0'=8,'sub_1'=2,'blk_0'=4,'blk_1'=8] {'blk_1'}, dimensions={0}, use_global_device_ids=true | all-gather | bytes 13824 | tf_op jit(solution)/shard_map/all_gather | solution.py:40
  851.2 29.4 %custom-call.11 = f32[64,5,5]{2,1,0:T(8,128)S(1)} custom-call(f32[64,5,5]{2,1,0:T(8,128)S(1)} %fusion), custom_call_target="Cholesky" | custom-call | tf_op jit(solution)/shard_map/jit(cholesky)/cholesky | solution.py:148
  (504 shorter events, 96.6 us)
Async XLA Ops:
  0.0 52.3 %copy-start = (bf16[1,2,64,2048]{3,2,1,0:T(8,128)(2,1)S(1)}, bf16[1,2,64,2048]{3,2,1,0:T(8,128)(2,1)}, u32[]{:S(2)}) copy-start(bf16[1,2,64,2048]{3,2,1,0:T(8,128)(2,1)} %param.16) | copy-start | bytes 1572868
  1.0 0.6 copy-start.21
  2.9 38.7 %all-to-all-start = ((bf16[32,2,64,128]{3,2,1,0:T(8,128)(2,1)}), bf16[32,2,64,128]{3,2,1,0:T(8,128)(2,1)S(1)}, u32[]{:S(2)}, u32[]{:S(2)}) async-start(bf16[32,2,64,128]{3,2,1,0:T(8,128)(2,1)} %broadcast_in_dim.37), calls=%async_computation | async-start | bytes 2097152 | tf_op jit(solution)/shard_map/all_to_all | solution.py:22
  18.3 167.1 %copy-start.30 = (pred[32]{0:T(512)(128)(4,1)}, pred[32]{0:T(512)(128)(4,1)S(1)}, u32[]{:S(2)}) copy-start(pred[32]{0:T(512)(128)(4,1)S(1)} %get-tuple-element.40) | copy-start | bytes 100
  19.1 168.9 %copy-start.25 = (pred[32]{0:T(512)(128)(4,1)}, pred[32]{0:T(512)(128)(4,1)S(1)}, u32[]{:S(2)}) copy-start(pred[32]{0:T(512)(128)(4,1)S(1)} %get-tuple-element.38) | copy-start | bytes 100
  19.1 165.7 %copy-start.39 = (s32[1024]{0:T(1024)}, s32[1024]{0:T(1024)S(1)}, u32[]{:S(2)}) copy-start(s32[1024]{0:T(1024)S(1)} %get-tuple-element.215) | copy-start | bytes 12292
  19.1 168.2 %copy-start.38 = (s32[1024]{0:T(1024)}, s32[1024]{0:T(1024)S(1)}, u32[]{:S(2)}) copy-start(s32[1024]{0:T(1024)S(1)} %get-tuple-element.216) | copy-start | bytes 12292
  46.1 8.0 collective-permute-start
  48.6 5.7 collective-permute-start.1
  49.9 1.0 copy-start.2
  51.0 1.0 copy-start.3
  52.3 1.0 copy-start.1
  54.4 0.7 copy-start.31
  56.4 5.3 copy-start.24
  56.4 32.4 %all-to-all-start.1 = ((bf16[32,2,64,128]{3,2,1,0:T(8,128)(2,1)}), bf16[32,2,64,128]{3,2,1,0:T(8,128)(2,1)S(1)}, u32[]{:S(2)}, u32[]{:S(2)}) async-start(bf16[32,2,64,128]{3,2,1,0:T(8,128)(2,1)} %broadcast_in_dim.38), calls=%async_computation.1 | async-start | bytes 2097152 | tf_op jit(solution)/shard_map/all_to_all | solution.py:22
  183.2 1.0 copy-start.9
  184.2 2.6 copy-start.5
  185.5 6.2 collective-permute-start.3
  188.1 3.9 collective-permute-start.2
  305.3 1.0 copy-start.10
  306.4 3.9 copy-start.6
  309.0 6.3 collective-permute-start.5
  310.8 0.7 copy-start.26
  311.7 3.9 collective-permute-start.4
  315.6 0.7 copy-start.32
  409.1 0.8 copy-start.40
  446.3 1.0 copy-start.11
  447.3 3.9 copy-start.7
  450.0 6.6 collective-permute-start.7
  451.3 1.4 copy-start.27
  451.8 4.2 copy-start.17
  452.8 4.5 collective-permute-start.6
  457.4 0.7 copy-start.33
  549.2 0.8 copy-start.37
  587.1 1.0 copy-start.12
  588.1 3.9 copy-start.8
  590.7 7.2 collective-permute-start.9
  592.0 1.4 copy-start.28
  592.6 4.0 copy-start.18
  593.6 5.1 collective-permute-start.8
  596.6 0.8 copy-start.15
  598.7 0.7 copy-start.34
  698.7 0.9 copy-start.36
  735.9 1.0 copy-start.13
  736.9 4.1 copy-start.4
  739.5 7.4 collective-permute-start.11
  741.1 1.4 copy-start.29
  741.6 4.0 copy-start.16
  742.6 5.1 collective-permute-start.10
  745.6 0.8 copy-start.14
  747.8 0.7 copy-start.35
  749.7 34.4 %all-to-all-start.11 = ((bf16[32,2,64,128]{3,2,1,0:T(8,128)(2,1)}), bf16[32,2,64,128]{3,2,1,0:T(8,128)(2,1)S(1)}, u32[]{:S(2)}, u32[]{:S(2)}) async-start(bf16[32,2,64,128]{3,2,1,0:T(8,128)(2,1)} %broadcast_in_dim.48), calls=%async_computation.11 | async-start | bytes 2097152 | tf_op jit(solution)/shard_map/all_to_all | solution.py:22
  755.6 0.7 copy-start.52
  756.2 0.7 copy-start.60
  756.2 5.4 copy-start.47
  757.6 0.7 copy-start.49
  760.2 0.7 copy-start.58
  761.6 0.7 copy-start.44
  761.6 0.7 copy-start.45
  761.6 0.7 copy-start.46
  785.8 0.8 copy-start.23
  849.3 0.7 copy-start.54
  880.8 0.9 copy-start.22
  880.8 0.9 copy-start.20
  (12 other events, 7.3 us)
